TPU v7x, 128 devices: a whole 4x4x4 slice. The times are simulated.
128 devices in a mesh: tm: 128 (over x, y, z, core).
Axes of the slice: x: 4, y: 4, z: 4, core: 2. Of those that a mesh axis runs over, the one named last changes fastest.
Arguments:
- stream: bfloat16 [262144, 64], P('tm'), may hold values from -6 to 6
- w_in: bfloat16 [64, 256], replicated, may hold values from -0.75 to 0.75
- w_conv: bfloat16 [4, 2, 256, 512], replicated, may hold values from -0.25 to 0.25
- w_residual: bfloat16 [3, 256, 256], replicated, may hold values from -0.375 to 0.375
- w_skip: bfloat16 [4, 256, 256], replicated, may hold values from -0.375 to 0.375
- w_out: bfloat16 [256, 64], replicated, may hold values from -0.375 to 0.375
- grad_pred: bfloat16 [262144, 64], P('tm'), may hold values from -0.01171875 to 0.01171875
Outputs:
- prediction: bfloat16 [262144, 64], P('tm')
- grad_w_in: float32 [64, 256], replicated
- grad_w_conv: float32 [4, 2, 256, 512], replicated
- grad_w_residual: float32 [3, 256, 256], replicated
- grad_w_skip: float32 [4, 256, 256], replicated
- grad_w_out: float32 [256, 64], replicated
All inputs are finite; a program needn't handle non-finite values.
Results may differ from a plain program's by a relative error of at most 0.012.
Values may be sent and summed in bfloat16 or wider, within the bound.
No kernel may reach another device: no remote copies, remote signals or barrier semaphores. Data moves between devices by JAX's collectives and lax.ppermute only.
A program may use at most 128 MiB of HBM per device.

v0:
```python
import functools
import jax
import jax.numpy as jnp
from jax import lax
from jax.experimental import pallas as pl
from jax.experimental.pallas import tpu as pltpu
from jax.sharding import Mesh, PartitionSpec as P

CHIPS = ("x", "y", "z")
ALL = ("x", "y", "z", "c")
BF = jnp.bfloat16
F32 = jnp.float32
LANES = 128
TILE = 16
GROUPS = 4
VMEM = pl.BlockSpec(memory_space=pltpu.VMEM)
SMEM = pl.BlockSpec(memory_space=pltpu.SMEM)
ANY = pl.BlockSpec(memory_space=pl.ANY)
HBM = pl.BlockSpec(memory_space=pltpu.HBM)


def grant(mib):
    return pltpu.CompilerParams(vmem_limit_bytes=mib * 2**20)


def dot(left, right):
    return jnp.dot(left, right, preferred_element_type=F32)


def dot_bt(left, right):
    return lax.dot_general(left, right, (((1,), (1,)), ((), ())), preferred_element_type=F32)


def dot_at(left, right):
    return lax.dot_general(left, right, (((0,), (0,)), ((), ())), preferred_element_type=F32)


def merge(left, right):
    def shift(v, by):
        flat = v.reshape(-1, LANES)
        return pltpu.roll(flat, by % flat.shape[0], 0).reshape(v.shape)

    low = lax.broadcasted_iota(jnp.int32, left.shape, left.ndim - 2) < 4
    return jnp.where(low, left, shift(right, 4)), jnp.where(low, shift(left, -4), right)


def regroup_kernel(stream_t, grad_t, sent, both, sems):
    feat = stream_t.shape[0]
    copies = [
        pltpu.make_async_copy(stream_t, both.at[:feat], sems.at[0]),
        pltpu.make_async_copy(grad_t, both.at[feat:], sems.at[1]),
    ]
    for copy in copies:
        copy.start()
    for copy in copies:
        copy.wait()
    x = both[...].astype(F32).T
    devices = sent.shape[0]
    x = x.reshape(4, devices // 2, 8, LANES)
    halves = []
    for k in range(2):
        even, odd = merge(x[2 * k], x[2 * k + 1])
        halves.append(jnp.stack([even, odd], axis=1))
    sent[...] = jnp.stack(halves, axis=2).reshape(sent.shape).astype(BF)


def step_kernel(
    mine_ref, got, w_in_at, w_conv_at, w_res_at, w_skip_at, w_out_at, keep_out, send_out,
    w_in, w_conv, w_res, w_skip, w_out_t, w_first, w_wide_t, xs, h0, h1, h2, h3, p_all, q_all, g_all, sd, dh, dz, joined, sems,
    *, layers, width, part, feat,
):
    rows = xs.shape[0]
    steps = rows // (TILE * GROUPS)
    hs = (h0, h1, h2, h3)
    mine = mine_ref[0]
    slots = (mine, 1 - mine)
    half_rows = joined.shape[1] * part
    top = h0.shape[0] - rows

    def put(row, value):
        n, done = value.shape[0], 0
        while done < n:
            half, inside = divmod(row + done, half_rows)
            chip, low = divmod(inside, part)
            take = min(part - low, n - done)
            joined[slots[half], chip, low : low + take, :] = value[done : done + take]
            done += take

    def put_slabs(row, value):
        for lane in range(0, value.shape[1], LANES):
            put(row, value[:, lane : lane + LANES].astype(BF))
            row += value.shape[0]
        return row

    def wrapped(tail, by):
        v = tail.astype(F32)
        v = pltpu.roll(v, by % v.shape[0], 0)
        row = lax.broadcasted_iota(jnp.int32, v.shape, 0) % TILE
        keep = row >= by if by > 0 else row < TILE + by
        return jnp.where(keep, v, 0.0).astype(BF)

    def fetch(source, to, at):
        copy = pltpu.make_async_copy(source, to, sems.at[at])
        copy.start()
        return copy

    ends = [fetch(w_in_at, w_in, 2), fetch(w_out_at, w_out_t, 3)]
    conv_copies = [fetch(w_conv_at.at[i], w_conv.at[i], 4 + i) for i in range(layers)]
    res_copy = fetch(w_res_at, w_res, 4 + layers)
    skip_copy = fetch(w_skip_at, w_skip, 5 + layers)

    g = [got[s].astype(F32).reshape(steps, 2, 8, LANES) for s in range(GROUPS)]
    pairs = [merge(g[2 * k], g[2 * k + 1]) for k in range(2)]
    even = jnp.stack([pairs[0][0], pairs[1][0]], axis=2)
    odd = jnp.stack([pairs[0][1], pairs[1][1]], axis=2)
    xs[...] = jnp.stack([even, odd], axis=2).reshape(rows, LANES).astype(BF)
    for copy in ends:
        copy.wait()
    none = jnp.zeros((feat, width), BF)
    w_first[:feat, :width] = w_in[...]
    w_first[feat:, :width] = none
    w_first[:feat, width:] = none
    w_first[feat:, width:] = w_out_t[...]
    w_wide_t[:feat, :] = w_out_t[...]
    w_wide_t[feat : 2 * feat, :] = none
    w_wide_t[2 * feat : 3 * feat, :] = none
    w_wide_t[3 * feat :, :] = w_out_t[...]
    h0[top:, :] = dot(xs[...], w_first[:, :width]).astype(BF)

    for layer in range(layers):
        h = hs[layer]
        lag = TILE * 2**layer
        h[top - lag : top] = wrapped(h[top + rows - lag :], 4)
        here = h[top:, :]
        conv_copies[layer].wait()
        if layer == 0:
            res_copy.wait()
        z = dot(h[top - lag : top - lag + rows, :], w_conv[layer, 0]) + dot(here, w_conv[layer, 1])
        a = jnp.tanh(z[:, :width])
        b = 0.5 * jnp.tanh(0.5 * z[:, width:]) + 0.5
        gate = a * b
        p_all[layer] = (b - a * gate).astype(BF)
        q_all[layer] = (gate - gate * b).astype(BF)
        gated = gate.astype(BF)
        g_all[:, layer * width : (layer + 1) * width] = gated
        if layer < layers - 1:
            hs[layer + 1][top:, :] = (here.astype(F32) + dot(gated, w_res[layer])).astype(BF)

    skip_copy.wait()
    skip = dot(g_all[...], w_skip[...].reshape(layers * width, width))
    s = 0.5 * jnp.tanh(0.5 * skip) + 0.5
    active = (skip * s).astype(BF)
    sd[:, :width] = (dot(xs[...], w_first[:, width:]) * s * (1.0 + skip * (1.0 - s))).astype(BF)
    both = dot_bt(active, w_wide_t[...])
    pa = both[:, :LANES].reshape(steps, 4, 2, 8, LANES)
    pb = both[:, LANES:].reshape(steps, 4, 2, 8, LANES)
    even, odd = merge(pa[:, 0] + pb[:, 2], pa[:, 1] + pb[:, 3])
    chips = joined.shape[1] // GROUPS
    for seg in range(GROUPS):
        from_seg = (even, odd)[seg % 2][:, seg // 2].reshape(chips, 2, 8, LANES)
        for core in range(2):
            rows8 = from_seg[:, core]
            tile = jnp.concatenate(
                [jnp.where(mine == 0, rows8, 0.0), jnp.where(mine == 1, rows8, 0.0)], axis=1
            )
            joined[slots[core], seg * chips : (seg + 1) * chips, part:, :] = tile.astype(BF)

    at_skip = layers * 4 * width * width // LANES
    at_res = at_skip + layers * width * width // LANES
    at_in = at_res + (layers - 1) * width * width // LANES
    at_out = at_in + feat * width // LANES
    end = put_slabs(at_out, dot_at(xs[...], active)[feat:, :])
    put(end, jnp.zeros((joined.shape[0] * half_rows - end, LANES), BF))

    for layer in reversed(range(layers)):
        h = hs[layer]
        lag = TILE * 2**layer
        last = layer == layers - 1
        dg = dot_bt(sd[:, :width], w_skip[layer])
        if not last:
            dg = dg + dot_bt(sd[:, width:], w_res[layer])
        dz[:rows, :width] = (dg * p_all[layer].astype(F32)).astype(BF)
        dz[:rows, width:] = (dg * q_all[layer].astype(F32)).astype(BF)
        gated = g_all[:, layer * width : (layer + 1) * width]
        side = dot_at(gated, sd[:, :width] if last else sd[...])
        put_slabs(at_skip + layer * width * width // LANES, side[:, :width])
        if not last:
            put_slabs(at_res + layer * width * width // LANES, side[:, width:])
        dz[rows : rows + lag] = wrapped(dz[:lag], -4)
        later = dz[lag : lag + rows]
        here = dz[:rows]
        grown = dot_bt(later, w_conv[layer, 0]) + dot_bt(here, w_conv[layer, 1])
        if not last:
            grown = grown + dh[...]
        dh[...] = grown
        sd[:, width:] = grown.astype(BF)
        row = layer * 4 * width * width // LANES
        row = put_slabs(row, dot_at(h[top:, :], later))
        put_slabs(row, dot_at(h[top:, :], here))

    put_slabs(at_in, dot_at(xs[...], sd[:, width:])[:feat, :])
    send = pltpu.make_async_copy(joined.at[1], send_out, sems.at[0])
    keep = pltpu.make_async_copy(joined.at[0], keep_out, sems.at[1])
    send.start()
    keep.start()
    send.wait()
    keep.wait()


def local_step(mine, got, w_in, w_conv, w_res, w_skip, w_out, chips, part):
    feat, width = w_in.shape
    layers = w_conv.shape[0]
    rows = got.shape[0] * got.shape[1]
    pad = TILE * 2 ** (layers - 1)
    flops = 2 * rows * width * (layers * (3 * 4 * width + 3 * 2 * width))
    half = jax.ShapeDtypeStruct((chips, part + TILE, LANES), BF)
    return pl.pallas_call(
        functools.partial(step_kernel, layers=layers, width=width, part=part, feat=feat),
        out_shape=(half, half),
        in_specs=[SMEM, VMEM] + [HBM] * 5,
        out_specs=(ANY, ANY),
        scratch_shapes=[
            pltpu.VMEM(w_in.shape, BF),
            pltpu.VMEM(w_conv.shape, BF),
            pltpu.VMEM(w_res.shape, BF),
            pltpu.VMEM(w_skip.shape, BF),
            pltpu.VMEM(w_out.shape[::-1], BF),
            pltpu.VMEM((LANES, 2 * width), BF),
            pltpu.VMEM((2 * LANES, width), BF),
            pltpu.VMEM((rows, LANES), BF),
        ]
        + [pltpu.VMEM((rows + pad, width), BF)] * layers
        + [
            pltpu.VMEM((layers, rows, width), BF),
            pltpu.VMEM((layers, rows, width), BF),
            pltpu.VMEM((rows, layers * width), BF),
            pltpu.VMEM((rows, 2 * width), BF),
            pltpu.VMEM((rows, width), F32),
            pltpu.VMEM((rows + pad, 2 * width), BF),
            pltpu.VMEM((2, chips, part + TILE, LANES), BF),
            pltpu.SemaphoreType.DMA((6 + layers,)),
        ],
        compiler_params=grant(46),
        cost_estimate=pl.CostEstimate(
            flops=flops, transcendentals=rows * width * 2 * layers, bytes_accessed=2**23
        ),
        name="residue_step",
    )(
        mine,
        got.reshape(GROUPS, -1, TILE, LANES),
        *(pltpu.with_memory_space_constraint(w, pltpu.HBM) for w in (w_in, w_conv, w_res, w_skip, w_out.T)),
    )


def total_kernel(out, spread, pred_t, *, part):
    chips = out.shape[0]
    total = jnp.sum(out[:, :part, :].astype(F32), axis=0).astype(BF)
    for chip in range(chips):
        spread[chip] = total
    rows = out[:, part:, :].astype(F32).reshape(chips, 2, 8, LANES)
    span = chips * 8
    for k, piece in enumerate(merge(rows[:, 0], rows[:, 1])):
        turned = piece.reshape(span, LANES).T
        for half in range(2):
            at = (2 * half + k) * span
            pred_t[:, at : at + span] = turned[half * 64 : half * 64 + 64].astype(BF)


def unpack_kernel(
    mine_ref, spread, theirs, conv_out, res_out, skip_out, in_out, out_out,
    conv, res, skip, first, last, sems,
    *, part,
):
    here = mine_ref[0] == 0
    half_rows = spread.shape[0] * part
    copies = []

    def piece(row, n):
        got = []
        while n > 0:
            half, inside = divmod(row, half_rows)
            chip, low = divmod(inside, part)
            take = min(part - low, n)
            a, b = spread[chip, low : low + take, :], theirs[chip, low : low + take, :]
            got.append(jnp.where(here, a, b) if half == 0 else jnp.where(here, b, a))
            row, n = row + take, n - take
        return got

    def fill(row, to):
        rows, cols = to.shape
        for lane in range(0, cols, LANES):
            at = 0
            for got in piece(row, rows):
                to[at : at + got.shape[0], lane : lane + LANES] = got.astype(F32)
                at += got.shape[0]
            row += rows
        return row

    def leave(scratch, out):
        copy = pltpu.make_async_copy(scratch, out, sems.at[len(copies)])
        copy.start()
        copies.append(copy)

    row = 0
    for layer in range(conv.shape[0]):
        for tap in range(2):
            row = fill(row, conv.at[layer, tap])
        leave(conv.at[layer], conv_out.at[layer])
    for kind, out in ((skip, skip_out), (res, res_out)):
        for layer in range(kind.shape[0]):
            row = fill(row, kind.at[layer])
        leave(kind, out)
    for kind, out in ((first, in_out), (last, out_out)):
        row = fill(row, kind)
        leave(kind, out)
    for copy in copies:
        copy.wait()


def body(stream, w_in, w_conv, w_res, w_skip, w_out, grad_pred):
    feat, width = w_in.shape
    rows = stream.shape[0]
    chips = lax.axis_size(CHIPS)
    devices = chips * lax.axis_size("c")
    sent = pl.pallas_call(
        regroup_kernel,
        out_shape=jax.ShapeDtypeStruct((devices, TILE, LANES), BF),
        in_specs=[HBM] * 2,
        out_specs=VMEM,
        scratch_shapes=[pltpu.VMEM((2 * feat, rows), BF), pltpu.SemaphoreType.DMA((2,))],
        compiler_params=grant(8),
        name="regroup",
    )(*(pltpu.with_memory_space_constraint(x.T, pltpu.HBM) for x in (stream, grad_pred)))
    got = lax.all_to_all(sent, ALL, 0, 0)
    mine = lax.axis_index("c")[None]
    swap = [(0, 1), (1, 0)]
    filled = (w_conv.size + w_res.size + w_skip.size + w_in.size + w_out.size) // LANES
    part = -(-filled // (devices * TILE)) * TILE
    kept, sent = local_step(mine, got, w_in, w_conv, w_res, w_skip, w_out, chips, part)
    away = lax.ppermute(sent, "c", swap)
    summed = (kept.astype(F32) + away.astype(F32)).astype(BF)
    out = lax.all_to_all(summed, CHIPS, 0, 0)
    spread, pred_t = pl.pallas_call(
        functools.partial(total_kernel, part=part),
        out_shape=(
            jax.ShapeDtypeStruct((chips, part, LANES), BF),
            jax.ShapeDtypeStruct((feat, rows), BF),
        ),
        in_specs=[VMEM],
        out_specs=(VMEM, VMEM),
        compiler_params=grant(10),
        name="total",
    )(out)
    spread = lax.all_to_all(spread, CHIPS, 0, 0)
    theirs = lax.ppermute(spread, "c", swap)
    shapes = [w_conv.shape, w_res.shape, w_skip.shape, w_in.shape, w_out.shape[::-1]]
    o_conv, o_res, o_skip, o_in, o_out_t = pl.pallas_call(
        functools.partial(unpack_kernel, part=part),
        out_shape=tuple(jax.ShapeDtypeStruct(s, F32) for s in shapes),
        in_specs=[SMEM, VMEM, VMEM],
        out_specs=(ANY,) * 5,
        scratch_shapes=[pltpu.VMEM(s, F32) for s in shapes]
        + [pltpu.SemaphoreType.DMA((w_conv.shape[0] + 4,))],
        compiler_params=grant(12),
        name="unpack",
    )(mine, spread, theirs)
    return pred_t.T, o_in, o_conv, o_res, o_skip, o_out_t.T


def solution(mesh):
    grid = Mesh(mesh.devices.reshape(4, 4, 4, 2), ALL)
    placed = (P(ALL, None), P(), P(), P(), P(), P(), P(ALL, None))
    return jax.shard_map(
        body,
        mesh=grid,
        in_specs=placed,
        out_specs=(P(ALL, None), P(), P(), P(), P(), P()),
        check_vma=False,
    )
```

profile of v0, /device:TPU:1, one launch (start us, length us, event | category | flops | bytes accessed | tf_op | source)
XLA Modules:
  0.0 127.7 jit_solution(797049123845042106)
XLA Ops:
  0.6 2.1 %regroup.1 = bf16[128,16,128]{2,1,0:T(8,128)(2,1)} custom-call(bf16[64,2048]{1,0:T(8,128)(2,1)} %bitcast.8, bf16[64,2048]{1,0:T(8,128)(2,1)} %bitcast.9), custom_call_target="tpu_custom_call" | custom-call | tf_op jit(solution)/shard_map/regroup/pallas_call | solution.py:325
  2.7 11.5 %all-to-all-start = ((bf16[128,16,128]{2,1,0:T(8,128)(2,1)}), bf16[128,16,128]{2,1,0:T(8,128)(2,1)S(1)}, u32[]{:S(2)}, u32[]{:S(2)}) async-start(bf16[128,16,128]{2,1,0:T(8,128)(2,1)} %regroup.1), calls=%async_computation | async-start | bytes 1048576 | tf_op jit(solution)/shard_map/all_to_all | solution.py:334
  14.2 13.5 %all-to-all-done = bf16[128,16,128]{2,1,0:T(8,128)(2,1)S(1)} async-done(((bf16[128,16,128]{2,1,0:T(8,128)(2,1)}), bf16[128,16,128]{2,1,0:T(8,128)(2,1)S(1)}, u32[]{:S(2)}, u32[]{:S(2)}) %all-to-all-start) | async-done | bytes 524320 | tf_op jit(solution)/shard_map/all_to_all | solution.py:334
  27.8 26.6 %residue_step.1 = (bf16[64,112,128]{2,1,0:T(8,128)(2,1)S(1)}, bf16[64,112,128]{2,1,0:T(8,128)(2,1)S(1)}) custom-call(s32[1]{0:T(128)} %bitcast.mine_ref, bf16[4,32,16,128]{3,2,1,0:T(8,128)(2,1)S(1)} %bitcast.7, bf16[64,256]{1,0:T(8,128)(2,1)} %w_in_at.1, bf16[4,2,256,512]{3,2,1,0:T(8,128)(2,1)} %w_conv_at.1, bf16[3,256,256]{2,1,0:T(8,128)(2,1)} %w_res_at.1, ...), custom_call_target="tpu_custom_call" | custom-call | flops 19327352832 | bytes 8388608 | tf_op jit(solution)/shard_map/residue_step/pallas_call | solution.py:217
  54.4 1.6 %collective-permute-start = (bf16[64,112,128]{2,1,0:T(8,128)(2,1)S(1)}, bf16[64,112,128]{2,1,0:T(8,128)(2,1)S(1)}, u32[]{:S(2)}, u32[]{:S(2)}) collective-permute-start(bf16[64,112,128]{2,1,0:T(8,128)(2,1)S(1)} %get-tuple-element.16), channel_id=1, source_target_pairs={{0,1},{1,0},{2,3},{3,2},{4,5},{5,4},{6,7},{7,6},{8,9},{9,8},{10,11... | collective-permute-start | bytes 5505032 | tf_op jit(solution)/shard_map/ppermute | solution.py:340
  55.9 3.4 %collective-permute-done = bf16[64,112,128]{2,1,0:T(8,128)(2,1)S(1)} collective-permute-done((bf16[64,112,128]{2,1,0:T(8,128)(2,1)S(1)}, bf16[64,112,128]{2,1,0:T(8,128)(2,1)S(1)}, u32[]{:S(2)}, u32[]{:S(2)}) %collective-permute-start) | collective-permute-done | bytes 1835040 | tf_op jit(solution)/shard_map/ppermute | solution.py:340
  59.3 0.5 add_convert_fusion
  59.8 29.6 %all_to_all.15.out = bf16[64,112,128]{2,1,0:T(8,128)(2,1)S(1)} all-to-all(bf16[64,112,128]{2,1,0:T(8,128)(2,1)S(1)} %add_convert_fusion), channel_id=1, replica_groups=mesh['x'=4,'y'=4,'z'=4,'c'=2] {'x','y','z'}, dimensions={0} | all-to-all | bytes 3670016 | tf_op jit(solution)/shard_map/all_to_all | solution.py:342
  89.4 0.9 total.1
  90.3 27.7 %all_to_all.16.spread = bf16[64,96,128]{2,1,0:T(8,128)(2,1)S(1)} all-to-all(bf16[64,96,128]{2,1,0:T(8,128)(2,1)S(1)} %get-tuple-element.18), channel_id=1, replica_groups=mesh['x'=4,'y'=4,'z'=4,'c'=2] {'x','y','z'}, dimensions={0} | all-to-all | bytes 3145728 | tf_op jit(solution)/shard_map/all_to_all | solution.py:354
  118.0 3.7 %collective-permute-start.1 = (bf16[64,96,128]{2,1,0:T(8,128)(2,1)S(1)}, bf16[64,96,128]{2,1,0:T(8,128)(2,1)S(1)}, u32[]{:S(2)}, u32[]{:S(2)}) collective-permute-start(bf16[64,96,128]{2,1,0:T(8,128)(2,1)S(1)} %all_to_all.16.spread), channel_id=1, source_target_pairs={{0,1},{1,0},{2,3},{3,2},{4,5},{5,4},{6,7},{7,6},{8,9},{9,8},{10,11... | collective-permute-start | bytes 4718600 | tf_op jit(solution)/shard_map/ppermute | solution.py:355
  121.7 3.0 %collective-permute-done.1.theirs = bf16[64,96,128]{2,1,0:T(8,128)(2,1)S(1)} collective-permute-done((bf16[64,96,128]{2,1,0:T(8,128)(2,1)S(1)}, bf16[64,96,128]{2,1,0:T(8,128)(2,1)S(1)}, u32[]{:S(2)}, u32[]{:S(2)}) %collective-permute-start.1) | collective-permute-done | bytes 1572896 | tf_op jit(solution)/shard_map/ppermute | solution.py:355
  124.7 2.8 %unpack.1 = (f32[4,2,256,512]{3,2,1,0:T(8,128)}, f32[3,256,256]{2,1,0:T(8,128)}, f32[4,256,256]{2,1,0:T(8,128)}, f32[64,256]{1,0:T(8,128)}, f32[64,256]{1,0:T(8,128)}) custom-call(s32[1]{0:T(128)} %bitcast.mine_ref, bf16[64,96,128]{2,1,0:T(8,128)(2,1)S(1)} %all_to_all.16.spread, bf16[64,96,128]{2,1,0:T(8,128)(2,1)S(1)} %collective-permute-done.1.theirs), custom_call_target="tpu_custom_call" | custom-call | tf_op jit(solution)/shard_map/unpack/pallas_call | solution.py:357
Async XLA Ops:
  2.7 25.0 %all-to-all-start = ((bf16[128,16,128]{2,1,0:T(8,128)(2,1)}), bf16[128,16,128]{2,1,0:T(8,128)(2,1)S(1)}, u32[]{:S(2)}, u32[]{:S(2)}) async-start(bf16[128,16,128]{2,1,0:T(8,128)(2,1)} %regroup.1), calls=%async_computation | async-start | bytes 1048576 | tf_op jit(solution)/shard_map/all_to_all | solution.py:334
  54.4 5.0 %collective-permute-start = (bf16[64,112,128]{2,1,0:T(8,128)(2,1)S(1)}, bf16[64,112,128]{2,1,0:T(8,128)(2,1)S(1)}, u32[]{:S(2)}, u32[]{:S(2)}) collective-permute-start(bf16[64,112,128]{2,1,0:T(8,128)(2,1)S(1)} %get-tuple-element.16), channel_id=1, source_target_pairs={{0,1},{1,0},{2,3},{3,2},{4,5},{5,4},{6,7},{7,6},{8,9},{9,8},{10,11... | collective-permute-start | bytes 5505032 | tf_op jit(solution)/shard_map/ppermute | solution.py:340
  118.0 6.7 %collective-permute-start.1 = (bf16[64,96,128]{2,1,0:T(8,128)(2,1)S(1)}, bf16[64,96,128]{2,1,0:T(8,128)(2,1)S(1)}, u32[]{:S(2)}, u32[]{:S(2)}) collective-permute-start(bf16[64,96,128]{2,1,0:T(8,128)(2,1)S(1)} %all_to_all.16.spread), channel_id=1, source_target_pairs={{0,1},{1,0},{2,3},{3,2},{4,5},{5,4},{6,7},{7,6},{8,9},{9,8},{10,11... | collective-permute-start | bytes 4718600 | tf_op jit(solution)/shard_map/ppermute | solution.py:355
where the time goes:
time: 128 us
  blocking collectives  57.3 us (45%)
  Pallas kernels  32.4 us (25%)
  waiting for transfers between devices  20 us (16%)
  starting transfers between devices  16.7 us (13%)
    all_to_all x1, blocking collectives, body(): out = lax.all_to_all(summed, CHIPS, 0, 0)  29.6 us
    all_to_all x1, blocking collectives, body(): spread = lax.all_to_all(spread, CHIPS, 0, 0)  27.7 us
    pallas_call x1, Pallas kernels, local_step(): pl.pallas_call(functools.partial(step_kernel, layers=layers, width=width,...  26.6 us
    all_to_all x1, waiting for transfers between devices, body(): got = lax.all_to_all(sent, ALL, 0, 0)  13.5 us
    all_to_all x1, starting transfers between devices, body(): got = lax.all_to_all(sent, ALL, 0, 0)  11.5 us
    ppermute x1, starting transfers between devices, body(): theirs = lax.ppermute(spread, 'c', swap)  3.66 us
    ppermute x1, waiting for transfers between devices, body(): away = lax.ppermute(sent, 'c', swap)  3.41 us
    ppermute x1, waiting for transfers between devices, body(): theirs = lax.ppermute(spread, 'c', swap)  3.04 us
  transfers between devices with their start and end apart: 3, of which 3 were waited for; matrix products, arithmetic and copies ran while one was open for 0% of the time, Pallas kernels for 0%

commit v1 on v0

--- a/solution.py
+++ b/solution.py
@@ -12,6 +12,7 @@
 F32 = jnp.float32
 LANES = 128
 TILE = 16
+SPLIT = 4
 GROUPS = 4
 VMEM = pl.BlockSpec(memory_space=pltpu.VMEM)
 SMEM = pl.BlockSpec(memory_space=pltpu.SMEM)
@@ -199,12 +200,18 @@
         put_slabs(row, dot_at(h[top:, :], here))
 
     put_slabs(at_in, dot_at(xs[...], sd[:, width:])[:feat, :])
-    send = pltpu.make_async_copy(joined.at[1], send_out, sems.at[0])
-    keep = pltpu.make_async_copy(joined.at[0], keep_out, sems.at[1])
-    send.start()
-    keep.start()
-    send.wait()
-    keep.wait()
+    last_copies = []
+    span = joined.shape[1] // SPLIT
+    for slot, to in ((1, send_out), (0, keep_out)):
+        for at in range(SPLIT):
+            some = pl.ds(at * span, span)
+            copy = pltpu.make_async_copy(
+                joined.at[slot, some], to.at[some], sems.at[6 + layers + slot * SPLIT + at]
+            )
+            copy.start()
+            last_copies.append(copy)
+    for copy in last_copies:
+        copy.wait()
 
 
 def local_step(mine, got, w_in, w_conv, w_res, w_skip, w_out, chips, part):
@@ -238,7 +245,7 @@
             pltpu.VMEM((rows, width), F32),
             pltpu.VMEM((rows + pad, 2 * width), BF),
             pltpu.VMEM((2, chips, part + TILE, LANES), BF),
-            pltpu.SemaphoreType.DMA((6 + layers,)),
+            pltpu.SemaphoreType.DMA((6 + layers + 2 * SPLIT,)),
         ],
         compiler_params=grant(46),
         cost_estimate=pl.CostEstimate(
@@ -266,55 +273,75 @@
             pred_t[:, at : at + span] = turned[half * 64 : half * 64 + 64].astype(BF)
 
 
-def unpack_kernel(
-    mine_ref, spread, theirs, conv_out, res_out, skip_out, in_out, out_out,
-    conv, res, skip, first, last, sems,
-    *, part,
-):
-    here = mine_ref[0] == 0
-    half_rows = spread.shape[0] * part
-    copies = []
-
-    def piece(row, n):
-        got = []
-        while n > 0:
-            half, inside = divmod(row, half_rows)
-            chip, low = divmod(inside, part)
-            take = min(part - low, n)
-            a, b = spread[chip, low : low + take, :], theirs[chip, low : low + take, :]
-            got.append(jnp.where(here, a, b) if half == 0 else jnp.where(here, b, a))
-            row, n = row + take, n - take
-        return got
+def unpack_kernel(mine_ref, piece, *refs, part, own):
+    conv_out, res_out, skip_out, in_out, out_out, conv, res, skip, first, last, sems = refs[-11:]
+    low = (mine_ref[0] == 0) if own else (mine_ref[0] == 1)
+    cut = piece.shape[0] * part
 
     def fill(row, to):
         rows, cols = to.shape
         for lane in range(0, cols, LANES):
             at = 0
-            for got in piece(row, rows):
-                to[at : at + got.shape[0], lane : lane + LANES] = got.astype(F32)
-                at += got.shape[0]
+            while at < rows:
+                chip, start = divmod(row + at, part)
+                take = min(part - start, rows - at)
+                to[at : at + take, lane : lane + LANES] = piece[chip, start : start + take, :].astype(F32)
+                at += take
             row += rows
         return row
 
-    def leave(scratch, out):
+    def leave(copies, scratch, out):
         copy = pltpu.make_async_copy(scratch, out, sems.at[len(copies)])
         copy.start()
         copies.append(copy)
 
-    row = 0
-    for layer in range(conv.shape[0]):
-        for tap in range(2):
-            row = fill(row, conv.at[layer, tap])
-        leave(conv.at[layer], conv_out.at[layer])
-    for kind, out in ((skip, skip_out), (res, res_out)):
-        for layer in range(kind.shape[0]):
-            row = fill(row, kind.at[layer])
-        leave(kind, out)
-    for kind, out in ((first, in_out), (last, out_out)):
-        row = fill(row, kind)
-        leave(kind, out)
-    for copy in copies:
-        copy.wait()
+    layers = conv.shape[0]
+    per_layer = 2 * conv.shape[2] * conv.shape[3] // LANES
+    low_layers = cut // per_layer
+    assert low_layers * per_layer == cut
+
+    @pl.when(low)
+    def _():
+        copies = []
+        row = 0
+        for layer in range(low_layers):
+            for tap in range(2):
+                row = fill(row, conv.at[layer, tap])
+            leave(copies, conv.at[layer], conv_out.at[layer])
+        for copy in copies:
+            copy.wait()
+
+    @pl.when(jnp.logical_not(low))
+    def _():
+        copies = []
+        row = 0
+        for layer in range(low_layers, layers):
+            for tap in range(2):
+                row = fill(row, conv.at[layer, tap])
+            leave(copies, conv.at[layer], conv_out.at[layer])
+        for kind, out in ((skip, skip_out), (res, res_out)):
+            for layer in range(kind.shape[0]):
+                row = fill(row, kind.at[layer])
+            leave(copies, kind, out)
+        for kind, out in ((first, in_out), (last, out_out)):
+            row = fill(row, kind)
+            leave(copies, kind, out)
+        for copy in copies:
+            copy.wait()
+
+
+def unpack(mine, piece, shapes, part, before=()):
+    return pl.pallas_call(
+        functools.partial(unpack_kernel, part=part, own=not before),
+        out_shape=tuple(jax.ShapeDtypeStruct(s, F32) for s in shapes),
+        in_specs=[SMEM, VMEM] + [ANY] * len(before),
+        out_specs=(ANY,) * len(shapes),
+        scratch_shapes=[pltpu.VMEM(s, F32) for s in shapes] + [pltpu.SemaphoreType.DMA((8,))],
+        input_output_aliases={2 + k: k for k in range(len(before))},
+        compiler_params=grant(12),
+        cost_estimate=pl.CostEstimate(flops=2**21, transcendentals=0, bytes_accessed=2**22),
+        name="unpack_rest" if before else "unpack_own",
+    )(mine, piece, *before)
 
 
 def body(stream, w_in, w_conv, w_res, w_skip, w_out, grad_pred):
@@ -331,8 +358,8 @@
         compiler_params=grant(8),
         name="regroup",
     )(*(pltpu.with_memory_space_constraint(x.T, pltpu.HBM) for x in (stream, grad_pred)))
+    mine, sent = lax.optimization_barrier((lax.axis_index("c")[None], sent))
     got = lax.all_to_all(sent, ALL, 0, 0)
-    mine = lax.axis_index("c")[None]
     swap = [(0, 1), (1, 0)]
     filled = (w_conv.size + w_res.size + w_skip.size + w_in.size + w_out.size) // LANES
     part = -(-filled // (devices * TILE)) * TILE
@@ -354,16 +381,8 @@
     spread = lax.all_to_all(spread, CHIPS, 0, 0)
     theirs = lax.ppermute(spread, "c", swap)
     shapes = [w_conv.shape, w_res.shape, w_skip.shape, w_in.shape, w_out.shape[::-1]]
-    o_conv, o_res, o_skip, o_in, o_out_t = pl.pallas_call(
-        functools.partial(unpack_kernel, part=part),
-        out_shape=tuple(jax.ShapeDtypeStruct(s, F32) for s in shapes),
-        in_specs=[SMEM, VMEM, VMEM],
-        out_specs=(ANY,) * 5,
-        scratch_shapes=[pltpu.VMEM(s, F32) for s in shapes]
-        + [pltpu.SemaphoreType.DMA((w_conv.shape[0] + 4,))],
-        compiler_params=grant(12),
-        name="unpack",
-    )(mine, spread, theirs)
+    own = unpack(mine, spread, shapes, part)
+    o_conv, o_res, o_skip, o_in, o_out_t = unpack(mine, theirs, shapes, part, own)
     return pred_t.T, o_in, o_conv, o_res, o_skip, o_out_t.T
 
 

time: 128 us -> 128 us (level)
  blocking collectives: 57.3 us -> 82.1 us
  waiting for transfers between devices: 20 us -> 4.65 us
  starting transfers between devices: 16.7 us -> 5.24 us
  Pallas kernels: 32.4 us -> 34.4 us
    all_to_all x0 -> x1, blocking collectives: none -> 24.8 us  [body(): got = lax.all_to_all(sent, ALL, 0, 0)]
    all_to_all x1 -> x0, waiting for transfers between devices: 13.5 us -> none  [body(): got = lax.all_to_all(sent, ALL, 0, 0)]
    all_to_all x1 -> x0, starting transfers between devices: 11.5 us -> none  [body(): got = lax.all_to_all(sent, ALL, 0, 0)]
    pallas_call x1, Pallas kernels: 26.6 us -> 28.6 us  [local_step(): pl.pallas_call(functools.partial(step_kernel, layers=layers, width=width,...]
    ppermute x1, waiting for transfers between devices: 3.04 us -> 1.23 us  [body(): theirs = lax.ppermute(spread, 'c', swap)]
    pallas_call x1 -> x2, Pallas kernels: 2.8 us -> 3.65 us  [unpack(): pl.pallas_call(functools.partial(unpack_kernel, part=part, own=not before...]
  transfers between devices with their start and end apart: 3 -> 2, of which waited for: 3 -> 2; matrix products, arithmetic and copies ran while one was open for 0% -> 0% of each run, Pallas kernels for 0% -> 1%
where the time goes in v1:
time: 128 us
  blocking collectives  82.1 us (64%)
  Pallas kernels  34.4 us (27%)
  starting transfers between devices  5.24 us (4%)
  waiting for transfers between devices  4.65 us (4%)
    all_to_all x1, blocking collectives, body(): out = lax.all_to_all(summed, CHIPS, 0, 0)  29.6 us
    pallas_call x1, Pallas kernels, local_step(): pl.pallas_call(functools.partial(step_kernel, layers=layers, width=width,...  28.6 us
    all_to_all x1, blocking collectives, body(): spread = lax.all_to_all(spread, CHIPS, 0, 0)  27.7 us
    all_to_all x1, blocking collectives, body(): got = lax.all_to_all(sent, ALL, 0, 0)  24.8 us
    ppermute x1, starting transfers between devices, body(): theirs = lax.ppermute(spread, 'c', swap)  3.66 us
    pallas_call x2, Pallas kernels, unpack(): pl.pallas_call(functools.partial(unpack_kernel, part=part, own=not before...  3.65 us
    ppermute x1, waiting for transfers between devices, body(): away = lax.ppermute(sent, 'c', swap)  3.41 us
  transfers between devices with their start and end apart: 2, of which 2 were waited for; matrix products, arithmetic and copies ran while one was open for 0% of the time, Pallas kernels for 1%

profile of v1, /device:TPU:1, one launch (start us, length us, event | category | flops | bytes accessed | tf_op | source)
XLA Modules:
  0.0 127.8 jit_solution(932301895476655524)
XLA Ops:
  0.6 1.3 %regroup.1 = bf16[128,16,128]{2,1,0:T(8,128)(2,1)S(1)} custom-call(bf16[64,2048]{1,0:T(8,128)(2,1)} %bitcast.8, bf16[64,2048]{1,0:T(8,128)(2,1)} %bitcast.9), custom_call_target="tpu_custom_call" | custom-call | tf_op jit(solution)/shard_map/regroup/pallas_call | solution.py:352
  2.0 24.8 %all_to_all.15 = bf16[128,16,128]{2,1,0:T(8,128)(2,1)S(1)} all-to-all(bf16[128,16,128]{2,1,0:T(8,128)(2,1)S(1)} %regroup.1), channel_id=1, replica_groups=mesh['x'=4,'y'=4,'z'=4,'c'=2] {'x','y','z','c'}, dimensions={0} | all-to-all | bytes 1048576 | tf_op jit(solution)/shard_map/all_to_all | solution.py:362
  26.8 28.6 %residue_step.1 = (bf16[64,112,128]{2,1,0:T(8,128)(2,1)S(1)}, bf16[64,112,128]{2,1,0:T(8,128)(2,1)S(1)}) custom-call(s32[1]{0:T(128)} %bitcast.mine_ref, bf16[4,32,16,128]{3,2,1,0:T(8,128)(2,1)S(1)} %bitcast.7, bf16[64,256]{1,0:T(8,128)(2,1)} %w_in_at.1, bf16[4,2,256,512]{3,2,1,0:T(8,128)(2,1)} %w_conv_at.1, bf16[3,256,256]{2,1,0:T(8,128)(2,1)} %w_res_at.1, ...), custom_call_target="tpu_custom_call" | custom-call | flops 19327352832 | bytes 8388608 | tf_op jit(solution)/shard_map/residue_step/pallas_call | solution.py:224
  55.4 1.6 %collective-permute-start = (bf16[64,112,128]{2,1,0:T(8,128)(2,1)S(1)}, bf16[64,112,128]{2,1,0:T(8,128)(2,1)S(1)}, u32[]{:S(2)}, u32[]{:S(2)}) collective-permute-start(bf16[64,112,128]{2,1,0:T(8,128)(2,1)S(1)} %get-tuple-element.25), channel_id=1, source_target_pairs={{0,1},{1,0},{2,3},{3,2},{4,5},{5,4},{6,7},{7,6},{8,9},{9,8},{10,11... | collective-permute-start | bytes 5505032 | tf_op jit(solution)/shard_map/ppermute | solution.py:367
  56.9 3.4 %collective-permute-done = bf16[64,112,128]{2,1,0:T(8,128)(2,1)S(1)} collective-permute-done((bf16[64,112,128]{2,1,0:T(8,128)(2,1)S(1)}, bf16[64,112,128]{2,1,0:T(8,128)(2,1)S(1)}, u32[]{:S(2)}, u32[]{:S(2)}) %collective-permute-start) | collective-permute-done | bytes 1835040 | tf_op jit(solution)/shard_map/ppermute | solution.py:367
  60.3 0.5 add_convert_fusion
  60.8 29.6 %all_to_all.16.out = bf16[64,112,128]{2,1,0:T(8,128)(2,1)S(1)} all-to-all(bf16[64,112,128]{2,1,0:T(8,128)(2,1)S(1)} %add_convert_fusion), channel_id=1, replica_groups=mesh['x'=4,'y'=4,'z'=4,'c'=2] {'x','y','z'}, dimensions={0} | all-to-all | bytes 3670016 | tf_op jit(solution)/shard_map/all_to_all | solution.py:369
  90.4 0.9 total.1
  91.3 27.7 %all_to_all.17.piece = bf16[64,96,128]{2,1,0:T(8,128)(2,1)S(1)} all-to-all(bf16[64,96,128]{2,1,0:T(8,128)(2,1)S(1)} %get-tuple-element.27), channel_id=1, replica_groups=mesh['x'=4,'y'=4,'z'=4,'c'=2] {'x','y','z'}, dimensions={0} | all-to-all | bytes 3145728 | tf_op jit(solution)/shard_map/all_to_all | solution.py:381
  119.0 3.7 %collective-permute-start.1 = (bf16[64,96,128]{2,1,0:T(8,128)(2,1)S(1)}, bf16[64,96,128]{2,1,0:T(8,128)(2,1)S(1)}, u32[]{:S(2)}, u32[]{:S(2)}) collective-permute-start(bf16[64,96,128]{2,1,0:T(8,128)(2,1)S(1)} %all_to_all.17.piece), channel_id=1, source_target_pairs={{0,1},{1,0},{2,3},{3,2},{4,5},{5,4},{6,7},{7,6},{8,9},{9,8},{10,11... | collective-permute-start | bytes 4718600 | tf_op jit(solution)/shard_map/ppermute | solution.py:382
  122.7 1.8 %unpack_own.1 = (f32[4,2,256,512]{3,2,1,0:T(8,128)}, f32[3,256,256]{2,1,0:T(8,128)}, f32[4,256,256]{2,1,0:T(8,128)}, f32[64,256]{1,0:T(8,128)}, f32[64,256]{1,0:T(8,128)}) custom-call(s32[1]{0:T(128)} %bitcast.mine_ref, bf16[64,96,128]{2,1,0:T(8,128)(2,1)S(1)} %all_to_all.17.piece), custom_call_target="tpu_custom_call" | custom-call | flops 2097152 | bytes 4194304 | tf_op jit(solution)/shard_map/unpack_own/pallas_call | solution.py:334
  124.5 1.2 collective-permute-done.1.piece
  125.7 1.9 %unpack_rest.1 = (f32[4,2,256,512]{3,2,1,0:T(8,128)}, f32[3,256,256]{2,1,0:T(8,128)}, f32[4,256,256]{2,1,0:T(8,128)}, f32[64,256]{1,0:T(8,128)}, f32[64,256]{1,0:T(8,128)}) custom-call(s32[1]{0:T(128)} %bitcast.mine_ref, ...), custom_call_target="tpu_custom_call", output_to_operand_aliasing={{0}: (2, {}), {1}: (3, {}), {2}: (4, {}), {3}: (5, {}), {4}... | custom-call | flops 2097152 | bytes 4194304 | tf_op jit(solution)/shard_map/unpack_rest/pallas_call | solution.py:334
Async XLA Ops:
  55.4 5.0 %collective-permute-start = (bf16[64,112,128]{2,1,0:T(8,128)(2,1)S(1)}, bf16[64,112,128]{2,1,0:T(8,128)(2,1)S(1)}, u32[]{:S(2)}, u32[]{:S(2)}) collective-permute-start(bf16[64,112,128]{2,1,0:T(8,128)(2,1)S(1)} %get-tuple-element.25), channel_id=1, source_target_pairs={{0,1},{1,0},{2,3},{3,2},{4,5},{5,4},{6,7},{7,6},{8,9},{9,8},{10,11... | collective-permute-start | bytes 5505032 | tf_op jit(solution)/shard_map/ppermute | solution.py:367
  119.0 6.7 %collective-permute-start.1 = (bf16[64,96,128]{2,1,0:T(8,128)(2,1)S(1)}, bf16[64,96,128]{2,1,0:T(8,128)(2,1)S(1)}, u32[]{:S(2)}, u32[]{:S(2)}) collective-permute-start(bf16[64,96,128]{2,1,0:T(8,128)(2,1)S(1)} %all_to_all.17.piece), channel_id=1, source_target_pairs={{0,1},{1,0},{2,3},{3,2},{4,5},{5,4},{6,7},{7,6},{8,9},{9,8},{10,11... | collective-permute-start | bytes 4718600 | tf_op jit(solution)/shard_map/ppermute | solution.py:382

commit v2 on v1

--- a/solution.py
+++ b/solution.py
@@ -12,7 +12,6 @@
 F32 = jnp.float32
 LANES = 128
 TILE = 16
-SPLIT = 4
 GROUPS = 4
 VMEM = pl.BlockSpec(memory_space=pltpu.VMEM)
 SMEM = pl.BlockSpec(memory_space=pltpu.SMEM)
@@ -45,13 +44,19 @@
     return jnp.where(low, left, shift(right, 4)), jnp.where(low, shift(left, -4), right)
 
 
-def regroup_kernel(stream_t, grad_t, sent, both, sems):
+def regroup_kernel(stream_t, grad_t, *refs):
+    both, sems = refs[-2:]
+    count = (len(refs) - 3) // 2
+    sent, fetched = refs[count], refs[count + 1 : -2]
     feat = stream_t.shape[0]
     copies = [
         pltpu.make_async_copy(stream_t, both.at[:feat], sems.at[0]),
         pltpu.make_async_copy(grad_t, both.at[feat:], sems.at[1]),
     ]
-    for copy in copies:
+    fetches = [
+        pltpu.make_async_copy(refs[k], fetched[k], sems.at[2 + k]) for k in range(count)
+    ]
+    for copy in copies + fetches:
         copy.start()
     for copy in copies:
         copy.wait()
@@ -63,11 +68,13 @@
         even, odd = merge(x[2 * k], x[2 * k + 1])
         halves.append(jnp.stack([even, odd], axis=1))
     sent[...] = jnp.stack(halves, axis=2).reshape(sent.shape).astype(BF)
+    for copy in fetches:
+        copy.wait()
 
 
 def step_kernel(
-    mine_ref, got, w_in_at, w_conv_at, w_res_at, w_skip_at, w_out_at, keep_out, send_out,
-    w_in, w_conv, w_res, w_skip, w_out_t, w_first, w_wide_t, xs, h0, h1, h2, h3, p_all, q_all, g_all, sd, dh, dz, joined, sems,
+    mine_ref, got, w_in, w_conv, w_res, w_skip, w_out_t, keep_out, send_out,
+    w_first, w_wide_t, xs, h0, h1, h2, h3, p_all, q_all, g_all, sd, dh, dz, joined, sems,
     *, layers, width, part, feat,
 ):
     rows = xs.shape[0]
@@ -100,23 +107,11 @@
         keep = row >= by if by > 0 else row < TILE + by
         return jnp.where(keep, v, 0.0).astype(BF)
 
-    def fetch(source, to, at):
-        copy = pltpu.make_async_copy(source, to, sems.at[at])
-        copy.start()
-        return copy
-
-    ends = [fetch(w_in_at, w_in, 2), fetch(w_out_at, w_out_t, 3)]
-    conv_copies = [fetch(w_conv_at.at[i], w_conv.at[i], 4 + i) for i in range(layers)]
-    res_copy = fetch(w_res_at, w_res, 4 + layers)
-    skip_copy = fetch(w_skip_at, w_skip, 5 + layers)
-
     g = [got[s].astype(F32).reshape(steps, 2, 8, LANES) for s in range(GROUPS)]
     pairs = [merge(g[2 * k], g[2 * k + 1]) for k in range(2)]
     even = jnp.stack([pairs[0][0], pairs[1][0]], axis=2)
     odd = jnp.stack([pairs[0][1], pairs[1][1]], axis=2)
     xs[...] = jnp.stack([even, odd], axis=2).reshape(rows, LANES).astype(BF)
-    for copy in ends:
-        copy.wait()
     none = jnp.zeros((feat, width), BF)
     w_first[:feat, :width] = w_in[...]
     w_first[feat:, :width] = none
@@ -133,9 +128,6 @@
         lag = TILE * 2**layer
         h[top - lag : top] = wrapped(h[top + rows - lag :], 4)
         here = h[top:, :]
-        conv_copies[layer].wait()
-        if layer == 0:
-            res_copy.wait()
         z = dot(h[top - lag : top - lag + rows, :], w_conv[layer, 0]) + dot(here, w_conv[layer, 1])
         a = jnp.tanh(z[:, :width])
         b = 0.5 * jnp.tanh(0.5 * z[:, width:]) + 0.5
@@ -147,7 +139,6 @@
         if layer < layers - 1:
             hs[layer + 1][top:, :] = (here.astype(F32) + dot(gated, w_res[layer])).astype(BF)
 
-    skip_copy.wait()
     skip = dot(g_all[...], w_skip[...].reshape(layers * width, width))
     s = 0.5 * jnp.tanh(0.5 * skip) + 0.5
     active = (skip * s).astype(BF)
@@ -200,21 +191,15 @@
         put_slabs(row, dot_at(h[top:, :], here))
 
     put_slabs(at_in, dot_at(xs[...], sd[:, width:])[:feat, :])
-    last_copies = []
-    span = joined.shape[1] // SPLIT
-    for slot, to in ((1, send_out), (0, keep_out)):
-        for at in range(SPLIT):
-            some = pl.ds(at * span, span)
-            copy = pltpu.make_async_copy(
-                joined.at[slot, some], to.at[some], sems.at[6 + layers + slot * SPLIT + at]
-            )
-            copy.start()
-            last_copies.append(copy)
-    for copy in last_copies:
-        copy.wait()
-
-
-def local_step(mine, got, w_in, w_conv, w_res, w_skip, w_out, chips, part):
+    send = pltpu.make_async_copy(joined.at[1], send_out, sems.at[0])
+    keep = pltpu.make_async_copy(joined.at[0], keep_out, sems.at[1])
+    send.start()
+    keep.start()
+    send.wait()
+    keep.wait()
+
+
+def local_step(mine, got, w_in, w_conv, w_res, w_skip, w_out_t, chips, part):
     feat, width = w_in.shape
     layers = w_conv.shape[0]
     rows = got.shape[0] * got.shape[1]
@@ -224,14 +209,9 @@
     return pl.pallas_call(
         functools.partial(step_kernel, layers=layers, width=width, part=part, feat=feat),
         out_shape=(half, half),
-        in_specs=[SMEM, VMEM] + [HBM] * 5,
+        in_specs=[SMEM] + [VMEM] * 6,
         out_specs=(ANY, ANY),
         scratch_shapes=[
-            pltpu.VMEM(w_in.shape, BF),
-            pltpu.VMEM(w_conv.shape, BF),
-            pltpu.VMEM(w_res.shape, BF),
-            pltpu.VMEM(w_skip.shape, BF),
-            pltpu.VMEM(w_out.shape[::-1], BF),
             pltpu.VMEM((LANES, 2 * width), BF),
             pltpu.VMEM((2 * LANES, width), BF),
             pltpu.VMEM((rows, LANES), BF),
@@ -245,9 +225,9 @@
             pltpu.VMEM((rows, width), F32),
             pltpu.VMEM((rows + pad, 2 * width), BF),
             pltpu.VMEM((2, chips, part + TILE, LANES), BF),
-            pltpu.SemaphoreType.DMA((6 + layers + 2 * SPLIT,)),
+            pltpu.SemaphoreType.DMA((2,)),
         ],
-        compiler_params=grant(46),
+        compiler_params=grant(42),
         cost_estimate=pl.CostEstimate(
             flops=flops, transcendentals=rows * width * 2 * layers, bytes_accessed=2**23
         ),
@@ -255,7 +235,11 @@
     )(
         mine,
         got.reshape(GROUPS, -1, TILE, LANES),
-        *(pltpu.with_memory_space_constraint(w, pltpu.HBM) for w in (w_in, w_conv, w_res, w_skip, w_out.T)),
+        w_in,
+        w_conv,
+        w_res,
+        w_skip,
+        w_out_t,
     )
 
 
@@ -349,21 +333,29 @@
     rows = stream.shape[0]
     chips = lax.axis_size(CHIPS)
     devices = chips * lax.axis_size("c")
-    sent = pl.pallas_call(
+    weights = (w_in, w_conv, w_res, w_skip, w_out.T)
+    sources = (stream.T, grad_pred.T, *weights)
+    sent, *weights = pl.pallas_call(
         regroup_kernel,
-        out_shape=jax.ShapeDtypeStruct((devices, TILE, LANES), BF),
-        in_specs=[HBM] * 2,
-        out_specs=VMEM,
-        scratch_shapes=[pltpu.VMEM((2 * feat, rows), BF), pltpu.SemaphoreType.DMA((2,))],
+        out_shape=(
+            jax.ShapeDtypeStruct((devices, TILE, LANES), BF),
+            *(jax.ShapeDtypeStruct(w.shape, BF) for w in weights),
+        ),
+        in_specs=[HBM] * len(sources),
+        out_specs=(VMEM, *(ANY for _ in weights)),
+        scratch_shapes=[
+            pltpu.VMEM((2 * feat, rows), BF),
+            pltpu.SemaphoreType.DMA((len(sources),)),
+        ],
         compiler_params=grant(8),
         name="regroup",
-    )(*(pltpu.with_memory_space_constraint(x.T, pltpu.HBM) for x in (stream, grad_pred)))
+    )(*(pltpu.with_memory_space_constraint(x, pltpu.HBM) for x in sources))
     mine, sent = lax.optimization_barrier((lax.axis_index("c")[None], sent))
     got = lax.all_to_all(sent, ALL, 0, 0)
     swap = [(0, 1), (1, 0)]
     filled = (w_conv.size + w_res.size + w_skip.size + w_in.size + w_out.size) // LANES
     part = -(-filled // (devices * TILE)) * TILE
-    kept, sent = local_step(mine, got, w_in, w_conv, w_res, w_skip, w_out, chips, part)
+    kept, sent = local_step(mine, got, *weights, chips, part)
     away = lax.ppermute(sent, "c", swap)
     summed = (kept.astype(F32) + away.astype(F32)).astype(BF)
     out = lax.all_to_all(summed, CHIPS, 0, 0)

time: 128 us -> 123 us (0.961)
  Pallas kernels: 34.4 us -> 30.1 us
    pallas_call x1, Pallas kernels: 28.6 us -> 23.5 us  [local_step(): pl.pallas_call(functools.partial(step_kernel, layers=layers, width=width,...]
where the time goes in v2:
time: 123 us
  blocking collectives  82.2 us (67%)
  Pallas kernels  30.1 us (24%)
  starting transfers between devices  4.99 us (4%)
  waiting for transfers between devices  4.65 us (4%)
    all_to_all x1, blocking collectives, body(): out = lax.all_to_all(summed, CHIPS, 0, 0)  29.6 us
    all_to_all x1, blocking collectives, body(): spread = lax.all_to_all(spread, CHIPS, 0, 0)  27.7 us
    all_to_all x1, blocking collectives, body(): got = lax.all_to_all(sent, ALL, 0, 0)  24.8 us
    pallas_call x1, Pallas kernels, local_step(): pl.pallas_call(functools.partial(step_kernel, layers=layers, width=width,...  23.5 us
    ppermute x1, starting transfers between devices, body(): theirs = lax.ppermute(spread, 'c', swap)  3.66 us
    pallas_call x2, Pallas kernels, unpack(): pl.pallas_call(functools.partial(unpack_kernel, part=part, own=not before...  3.65 us
    ppermute x1, waiting for transfers between devices, body(): away = lax.ppermute(sent, 'c', swap)  3.41 us
  transfers between devices with their start and end apart: 2, of which 2 were waited for; matrix products, arithmetic and copies ran while one was open for 0% of the time, Pallas kernels for 1%

profile of v2, /device:TPU:1, one launch (start us, length us, event | category | flops | bytes accessed | tf_op | source)
XLA Modules:
  0.0 123.2 jit_solution(16895241484711059110)
XLA Ops:
  0.6 2.0 %regroup.1 = (bf16[128,16,128]{2,1,0:T(8,128)(2,1)S(1)}, bf16[64,256]{1,0:T(8,128)(2,1)S(1)}, bf16[4,2,256,512]{3,2,1,0:T(8,128)(2,1)S(1)}, bf16[3,256,256]{2,1,...) custom-call(bf16[64,2048]{1,0:T(8,128)(2,1)} %bitcast.8, bf16[64,2048]{1,0:T(8,128)(2,1)} %bitcast.9, ...), custom_call_target="tpu_custom_call" | custom-call | tf_op jit(solution)/shard_map/regroup/pallas_call | solution.py:338
  2.7 24.8 %all_to_all.15 = bf16[128,16,128]{2,1,0:T(8,128)(2,1)S(1)} all-to-all(bf16[128,16,128]{2,1,0:T(8,128)(2,1)S(1)} %get-tuple-element.30), channel_id=1, replica_groups=mesh['x'=4,'y'=4,'z'=4,'c'=2] {'x','y','z','c'}, dimensions={0} | all-to-all | bytes 1048576 | tf_op jit(solution)/shard_map/all_to_all | solution.py:354
  27.5 23.5 %residue_step.1 = (bf16[64,112,128]{2,1,0:T(8,128)(2,1)S(1)}, bf16[64,112,128]{2,1,0:T(8,128)(2,1)S(1)}) custom-call(s32[1]{0:T(128)} %bitcast.mine_ref, bf16[4,32,16,128]{3,2,1,0:T(8,128)(2,1)S(1)} %bitcast.7, bf16[64,256]{1,0:T(8,128)(2,1)S(1)} %get-tuple-element.31.w_in, bf16[4,2,256,512]{3,2,1,0:T(8,128)(2,1)S(1)} %get-tuple-element.32.w_conv, ...), custom_call_target="tpu_custom_call" | custom-call | flops 19327352832 | bytes 8388608 | tf_op jit(solution)/shard_map/residue_step/pallas_call | solution.py:209
  51.0 1.3 %collective-permute-start = (bf16[64,112,128]{2,1,0:T(8,128)(2,1)S(1)}, bf16[64,112,128]{2,1,0:T(8,128)(2,1)S(1)}, u32[]{:S(2)}, u32[]{:S(2)}) collective-permute-start(bf16[64,112,128]{2,1,0:T(8,128)(2,1)S(1)} %get-tuple-element.37), channel_id=1, source_target_pairs={{0,1},{1,0},{2,3},{3,2},{4,5},{5,4},{6,7},{7,6},{8,9},{9,8},{10,11... | collective-permute-start | bytes 5505032 | tf_op jit(solution)/shard_map/ppermute | solution.py:359
  52.4 3.4 %collective-permute-done = bf16[64,112,128]{2,1,0:T(8,128)(2,1)S(1)} collective-permute-done((bf16[64,112,128]{2,1,0:T(8,128)(2,1)S(1)}, bf16[64,112,128]{2,1,0:T(8,128)(2,1)S(1)}, u32[]{:S(2)}, u32[]{:S(2)}) %collective-permute-start) | collective-permute-done | bytes 1835040 | tf_op jit(solution)/shard_map/ppermute | solution.py:359
  55.8 0.5 add_convert_fusion
  56.2 29.6 %all_to_all.16.out = bf16[64,112,128]{2,1,0:T(8,128)(2,1)S(1)} all-to-all(bf16[64,112,128]{2,1,0:T(8,128)(2,1)S(1)} %add_convert_fusion), channel_id=1, replica_groups=mesh['x'=4,'y'=4,'z'=4,'c'=2] {'x','y','z'}, dimensions={0} | all-to-all | bytes 3670016 | tf_op jit(solution)/shard_map/all_to_all | solution.py:361
  85.9 0.9 total.1
  86.7 27.7 %all_to_all.17.piece = bf16[64,96,128]{2,1,0:T(8,128)(2,1)S(1)} all-to-all(bf16[64,96,128]{2,1,0:T(8,128)(2,1)S(1)} %get-tuple-element.39), channel_id=1, replica_groups=mesh['x'=4,'y'=4,'z'=4,'c'=2] {'x','y','z'}, dimensions={0} | all-to-all | bytes 3145728 | tf_op jit(solution)/shard_map/all_to_all | solution.py:373
  114.5 3.7 %collective-permute-start.1 = (bf16[64,96,128]{2,1,0:T(8,128)(2,1)S(1)}, bf16[64,96,128]{2,1,0:T(8,128)(2,1)S(1)}, u32[]{:S(2)}, u32[]{:S(2)}) collective-permute-start(bf16[64,96,128]{2,1,0:T(8,128)(2,1)S(1)} %all_to_all.17.piece), channel_id=1, source_target_pairs={{0,1},{1,0},{2,3},{3,2},{4,5},{5,4},{6,7},{7,6},{8,9},{9,8},{10,11... | collective-permute-start | bytes 4718600 | tf_op jit(solution)/shard_map/ppermute | solution.py:374
  118.1 1.8 %unpack_own.1 = (f32[4,2,256,512]{3,2,1,0:T(8,128)}, f32[3,256,256]{2,1,0:T(8,128)}, f32[4,256,256]{2,1,0:T(8,128)}, f32[64,256]{1,0:T(8,128)}, f32[64,256]{1,0:T(8,128)}) custom-call(s32[1]{0:T(128)} %bitcast.mine_ref, bf16[64,96,128]{2,1,0:T(8,128)(2,1)S(1)} %all_to_all.17.piece), custom_call_target="tpu_custom_call" | custom-call | flops 2097152 | bytes 4194304 | tf_op jit(solution)/shard_map/unpack_own/pallas_call | solution.py:318
  119.9 1.2 %collective-permute-done.1.piece = bf16[64,96,128]{2,1,0:T(8,128)(2,1)S(1)} collective-permute-done((bf16[64,96,128]{2,1,0:T(8,128)(2,1)S(1)}, bf16[64,96,128]{2,1,0:T(8,128)(2,1)S(1)}, u32[]{:S(2)}, u32[]{:S(2)}) %collective-permute-start.1) | collective-permute-done | bytes 1572896 | tf_op jit(solution)/shard_map/ppermute | solution.py:374
  121.2 1.9 %unpack_rest.1 = (f32[4,2,256,512]{3,2,1,0:T(8,128)}, f32[3,256,256]{2,1,0:T(8,128)}, f32[4,256,256]{2,1,0:T(8,128)}, f32[64,256]{1,0:T(8,128)}, f32[64,256]{1,0:T(8,128)}) custom-call(s32[1]{0:T(128)} %bitcast.mine_ref, ...), custom_call_target="tpu_custom_call", output_to_operand_aliasing={{0}: (2, {}), {1}: (3, {}), {2}: (4, {}), {3}: (5, {}), {4}... | custom-call | flops 2097152 | bytes 4194304 | tf_op jit(solution)/shard_map/unpack_rest/pallas_call | solution.py:318
Async XLA Ops:
  51.0 4.7 %collective-permute-start = (bf16[64,112,128]{2,1,0:T(8,128)(2,1)S(1)}, bf16[64,112,128]{2,1,0:T(8,128)(2,1)S(1)}, u32[]{:S(2)}, u32[]{:S(2)}) collective-permute-start(bf16[64,112,128]{2,1,0:T(8,128)(2,1)S(1)} %get-tuple-element.37), channel_id=1, source_target_pairs={{0,1},{1,0},{2,3},{3,2},{4,5},{5,4},{6,7},{7,6},{8,9},{9,8},{10,11... | collective-permute-start | bytes 5505032 | tf_op jit(solution)/shard_map/ppermute | solution.py:359
  114.5 6.7 %collective-permute-start.1 = (bf16[64,96,128]{2,1,0:T(8,128)(2,1)S(1)}, bf16[64,96,128]{2,1,0:T(8,128)(2,1)S(1)}, u32[]{:S(2)}, u32[]{:S(2)}) collective-permute-start(bf16[64,96,128]{2,1,0:T(8,128)(2,1)S(1)} %all_to_all.17.piece), channel_id=1, source_target_pairs={{0,1},{1,0},{2,3},{3,2},{4,5},{5,4},{6,7},{7,6},{8,9},{9,8},{10,11... | collective-permute-start | bytes 4718600 | tf_op jit(solution)/shard_map/ppermute | solution.py:374

commit v3 on v2

--- a/solution.py
+++ b/solution.py
@@ -243,11 +243,15 @@
     )
 
 
-def total_kernel(out, spread, pred_t, *, part):
+def total_kernel(out, spread, *, part):
     chips = out.shape[0]
     total = jnp.sum(out[:, :part, :].astype(F32), axis=0).astype(BF)
     for chip in range(chips):
         spread[chip] = total
+
+
+def place_prediction(out, pred_t, part):
+    chips = out.shape[0]
     rows = out[:, part:, :].astype(F32).reshape(chips, 2, 8, LANES)
     span = chips * 8
     for k, piece in enumerate(merge(rows[:, 0], rows[:, 1])):
@@ -258,6 +262,9 @@
 
 
 def unpack_kernel(mine_ref, piece, *refs, part, own):
+    if own:
+        place_prediction(refs[0], refs[6], part)
+        refs = refs[:6] + refs[7:]
     conv_out, res_out, skip_out, in_out, out_out, conv, res, skip, first, last, sems = refs[-11:]
     low = (mine_ref[0] == 0) if own else (mine_ref[0] == 1)
     cut = piece.shape[0] * part
@@ -314,18 +321,18 @@
             copy.wait()
 
 
-def unpack(mine, piece, shapes, part, before=()):
+def unpack(mine, piece, shapes, part, before=(), received=(), pred=()):
     return pl.pallas_call(
         functools.partial(unpack_kernel, part=part, own=not before),
-        out_shape=tuple(jax.ShapeDtypeStruct(s, F32) for s in shapes),
-        in_specs=[SMEM, VMEM] + [ANY] * len(before),
-        out_specs=(ANY,) * len(shapes),
+        out_shape=tuple(jax.ShapeDtypeStruct(s, F32) for s in shapes) + pred,
+        in_specs=[SMEM, VMEM] + [VMEM] * len(received) + [ANY] * len(before),
+        out_specs=(ANY,) * len(shapes) + (VMEM,) * len(pred),
         scratch_shapes=[pltpu.VMEM(s, F32) for s in shapes] + [pltpu.SemaphoreType.DMA((8,))],
         input_output_aliases={2 + k: k for k in range(len(before))},
         compiler_params=grant(12),
         cost_estimate=pl.CostEstimate(flops=2**21, transcendentals=0, bytes_accessed=2**22),
         name="unpack_rest" if before else "unpack_own",
-    )(mine, piece, *before)
+    )(mine, piece, *received, *before)
 
 
 def body(stream, w_in, w_conv, w_res, w_skip, w_out, grad_pred):
@@ -359,21 +366,19 @@
     away = lax.ppermute(sent, "c", swap)
     summed = (kept.astype(F32) + away.astype(F32)).astype(BF)
     out = lax.all_to_all(summed, CHIPS, 0, 0)
-    spread, pred_t = pl.pallas_call(
+    spread = pl.pallas_call(
         functools.partial(total_kernel, part=part),
-        out_shape=(
-            jax.ShapeDtypeStruct((chips, part, LANES), BF),
-            jax.ShapeDtypeStruct((feat, rows), BF),
-        ),
+        out_shape=jax.ShapeDtypeStruct((chips, part, LANES), BF),
         in_specs=[VMEM],
-        out_specs=(VMEM, VMEM),
+        out_specs=VMEM,
         compiler_params=grant(10),
         name="total",
     )(out)
     spread = lax.all_to_all(spread, CHIPS, 0, 0)
     theirs = lax.ppermute(spread, "c", swap)
     shapes = [w_conv.shape, w_res.shape, w_skip.shape, w_in.shape, w_out.shape[::-1]]
-    own = unpack(mine, spread, shapes, part)
+    pred = (jax.ShapeDtypeStruct((feat, rows), BF),)
+    *own, pred_t = unpack(mine, spread, shapes, part, received=(out,), pred=pred)
     o_conv, o_res, o_skip, o_in, o_out_t = unpack(mine, theirs, shapes, part, own)
     return pred_t.T, o_in, o_conv, o_res, o_skip, o_out_t.T
 

time: 123 us -> 123 us (level)
  transfers between devices with their start and end apart: 2 -> 2, of which waited for: 2 -> 2; matrix products, arithmetic and copies ran while one was open for 0% -> 0% of each run, Pallas kernels for 1% -> 2%
where the time goes in v3:
time: 123 us
  blocking collectives  82.2 us (67%)
  Pallas kernels  30.3 us (25%)
  starting transfers between devices  4.99 us (4%)
  waiting for transfers between devices  3.78 us (3%)
    all_to_all x1, blocking collectives, body(): out = lax.all_to_all(summed, CHIPS, 0, 0)  29.6 us
    all_to_all x1, blocking collectives, body(): spread = lax.all_to_all(spread, CHIPS, 0, 0)  27.7 us
    all_to_all x1, blocking collectives, body(): got = lax.all_to_all(sent, ALL, 0, 0)  24.8 us
    pallas_call x1, Pallas kernels, local_step(): pl.pallas_call(functools.partial(step_kernel, layers=layers, width=width,...  23.5 us
    pallas_call x2, Pallas kernels, unpack(): pl.pallas_call(functools.partial(unpack_kernel, part=part, own=not before...  4.51 us
    ppermute x1, starting transfers between devices, body(): theirs = lax.ppermute(spread, 'c', swap)  3.66 us
    ppermute x1, waiting for transfers between devices, body(): away = lax.ppermute(sent, 'c', swap)  3.41 us
  transfers between devices with their start and end apart: 2, of which 2 were waited for; matrix products, arithmetic and copies ran while one was open for 0% of the time, Pallas kernels for 2%

profile of v3, /device:TPU:1, one launch (start us, length us, event | category | flops | bytes accessed | tf_op | source)
XLA Modules:
  0.0 122.6 jit_solution(18192275822786238473)
XLA Ops:
  0.6 2.0 %regroup.1 = (bf16[128,16,128]{2,1,0:T(8,128)(2,1)S(1)}, bf16[64,256]{1,0:T(8,128)(2,1)S(1)}, bf16[4,2,256,512]{3,2,1,0:T(8,128)(2,1)S(1)}, bf16[3,256,256]{2,1,...) custom-call(bf16[64,2048]{1,0:T(8,128)(2,1)} %bitcast.8, bf16[64,2048]{1,0:T(8,128)(2,1)} %bitcast.9, ...), custom_call_target="tpu_custom_call" | custom-call | tf_op jit(solution)/shard_map/regroup/pallas_call | solution.py:345
  2.7 24.8 %all_to_all.15 = bf16[128,16,128]{2,1,0:T(8,128)(2,1)S(1)} all-to-all(bf16[128,16,128]{2,1,0:T(8,128)(2,1)S(1)} %get-tuple-element.29), channel_id=1, replica_groups=mesh['x'=4,'y'=4,'z'=4,'c'=2] {'x','y','z','c'}, dimensions={0} | all-to-all | bytes 1048576 | tf_op jit(solution)/shard_map/all_to_all | solution.py:361
  27.5 23.5 %residue_step.1 = (bf16[64,112,128]{2,1,0:T(8,128)(2,1)S(1)}, bf16[64,112,128]{2,1,0:T(8,128)(2,1)S(1)}) custom-call(s32[1]{0:T(128)} %bitcast.mine_ref, bf16[4,32,16,128]{3,2,1,0:T(8,128)(2,1)S(1)} %bitcast.7, bf16[64,256]{1,0:T(8,128)(2,1)S(1)} %get-tuple-element.30.w_in, bf16[4,2,256,512]{3,2,1,0:T(8,128)(2,1)S(1)} %get-tuple-element.31.w_conv, ...), custom_call_target="tpu_custom_call" | custom-call | flops 19327352832 | bytes 8388608 | tf_op jit(solution)/shard_map/residue_step/pallas_call | solution.py:209
  51.0 1.3 %collective-permute-start = (bf16[64,112,128]{2,1,0:T(8,128)(2,1)S(1)}, bf16[64,112,128]{2,1,0:T(8,128)(2,1)S(1)}, u32[]{:S(2)}, u32[]{:S(2)}) collective-permute-start(bf16[64,112,128]{2,1,0:T(8,128)(2,1)S(1)} %get-tuple-element.36), channel_id=1, source_target_pairs={{0,1},{1,0},{2,3},{3,2},{4,5},{5,4},{6,7},{7,6},{8,9},{9,8},{10,11... | collective-permute-start | bytes 5505032 | tf_op jit(solution)/shard_map/ppermute | solution.py:366
  52.4 3.4 %collective-permute-done = bf16[64,112,128]{2,1,0:T(8,128)(2,1)S(1)} collective-permute-done((bf16[64,112,128]{2,1,0:T(8,128)(2,1)S(1)}, bf16[64,112,128]{2,1,0:T(8,128)(2,1)S(1)}, u32[]{:S(2)}, u32[]{:S(2)}) %collective-permute-start) | collective-permute-done | bytes 1835040 | tf_op jit(solution)/shard_map/ppermute | solution.py:366
  55.8 0.5 add_convert_fusion
  56.2 29.6 %all_to_all.16.out.refs_0_ = bf16[64,112,128]{2,1,0:T(8,128)(2,1)S(1)} all-to-all(bf16[64,112,128]{2,1,0:T(8,128)(2,1)S(1)} %add_convert_fusion), channel_id=1, replica_groups=mesh['x'=4,'y'=4,'z'=4,'c'=2] {'x','y','z'}, dimensions={0} | all-to-all | bytes 3670016 | tf_op jit(solution)/shard_map/all_to_all | solution.py:368
  85.9 0.3 total.1
  86.1 27.7 %all_to_all.17.piece = bf16[64,96,128]{2,1,0:T(8,128)(2,1)S(1)} all-to-all(bf16[64,96,128]{2,1,0:T(8,128)(2,1)S(1)} %total.1), channel_id=1, replica_groups=mesh['x'=4,'y'=4,'z'=4,'c'=2] {'x','y','z'}, dimensions={0} | all-to-all | bytes 3145728 | tf_op jit(solution)/shard_map/all_to_all | solution.py:377
  113.9 3.7 %collective-permute-start.1 = (bf16[64,96,128]{2,1,0:T(8,128)(2,1)S(1)}, bf16[64,96,128]{2,1,0:T(8,128)(2,1)S(1)}, u32[]{:S(2)}, u32[]{:S(2)}) collective-permute-start(bf16[64,96,128]{2,1,0:T(8,128)(2,1)S(1)} %all_to_all.17.piece), channel_id=1, source_target_pairs={{0,1},{1,0},{2,3},{3,2},{4,5},{5,4},{6,7},{7,6},{8,9},{9,8},{10,11... | collective-permute-start | bytes 4718600 | tf_op jit(solution)/shard_map/ppermute | solution.py:378
  117.5 2.7 %unpack_own.1 = (f32[4,2,256,512]{3,2,1,0:T(8,128)}, f32[3,256,256]{2,1,0:T(8,128)}, f32[4,256,256]{2,1,0:T(8,128)}, f32[64,256]{1,0:T(8,128)}, f32[64,256]{1,0:T(8,128)}, /*index=5*/bf16[64,2048]{1,0:T(8,128)(2,1)}) custom-call(s32[1]{0:T(128)} %bitcast.mine_ref, bf16[64,96,128]{2,1,0:T(8,128)(2,1)S(1)} %all_to_all.17.piece, ...), custom_call_target="tpu_custom_call" | custom-call | flops 2097152 | bytes 4194304 | tf_op jit(solution)/shard_map/unpack_own/pallas_call | solution.py:325
  120.2 0.4 collective-permute-done.1.piece
  120.6 1.9 %unpack_rest.1 = (f32[4,2,256,512]{3,2,1,0:T(8,128)}, f32[3,256,256]{2,1,0:T(8,128)}, f32[4,256,256]{2,1,0:T(8,128)}, f32[64,256]{1,0:T(8,128)}, f32[64,256]{1,0:T(8,128)}) custom-call(s32[1]{0:T(128)} %bitcast.mine_ref, ...), custom_call_target="tpu_custom_call", output_to_operand_aliasing={{0}: (2, {}), {1}: (3, {}), {2}: (4, {}), {3}: (5, {}), {4}... | custom-call | flops 2097152 | bytes 4194304 | tf_op jit(solution)/shard_map/unpack_rest/pallas_call | solution.py:325
Async XLA Ops:
  51.0 4.7 %collective-permute-start = (bf16[64,112,128]{2,1,0:T(8,128)(2,1)S(1)}, bf16[64,112,128]{2,1,0:T(8,128)(2,1)S(1)}, u32[]{:S(2)}, u32[]{:S(2)}) collective-permute-start(bf16[64,112,128]{2,1,0:T(8,128)(2,1)S(1)} %get-tuple-element.36), channel_id=1, source_target_pairs={{0,1},{1,0},{2,3},{3,2},{4,5},{5,4},{6,7},{7,6},{8,9},{9,8},{10,11... | collective-permute-start | bytes 5505032 | tf_op jit(solution)/shard_map/ppermute | solution.py:366
  113.9 6.7 %collective-permute-start.1 = (bf16[64,96,128]{2,1,0:T(8,128)(2,1)S(1)}, bf16[64,96,128]{2,1,0:T(8,128)(2,1)S(1)}, u32[]{:S(2)}, u32[]{:S(2)}) collective-permute-start(bf16[64,96,128]{2,1,0:T(8,128)(2,1)S(1)} %all_to_all.17.piece), channel_id=1, source_target_pairs={{0,1},{1,0},{2,3},{3,2},{4,5},{5,4},{6,7},{7,6},{8,9},{9,8},{10,11... | collective-permute-start | bytes 4718600 | tf_op jit(solution)/shard_map/ppermute | solution.py:378
